TPU v7x, 32 devices: a 4x4x1 block of a 4x4x8 slice. The times are simulated.
32 devices in a mesh: dp: 2 (over z, core), sp: 16 (over x, y).
Axes of the slice: x: 4, y: 4, z: 1, core: 2. Of those that a mesh axis runs over, the one named last changes fastest.
The devices are a block of a 4x4x8 slice.
Arguments:
- q: bfloat16 [64, 64, 112], P('dp'), parts along dimension 0
- k: bfloat16 [64, 2048, 64, 112], P('dp', 'sp'), parts along dimension 0
- v: bfloat16 [64, 2048, 64, 112], P('dp', 'sp'), parts along dimension 0
Outputs:
- q: bfloat16 [64, 64, 112], P('dp'), parts along dimension 0
There are 2 independent parts. A program takes and returns all parts, laid end to end along the dimension named above; each array names one.
All inputs are finite; a program needn't handle non-finite values.
Results may differ from a plain program's by a relative error of at most 0.012.
Values are sent between devices in bfloat16 or wider.
A program may use at most 768 MiB of HBM per device.

v0:
```python
import jax
import jax.numpy as jnp
from jax import lax
from jax.sharding import PartitionSpec as P


def einsum(form, a, b):
    return jnp.einsum(form, a.astype(jnp.float32), b.astype(jnp.float32))


def part_of(q, k, v):
    grouped = q.reshape(q.shape[0], k.shape[2], -1, q.shape[2])
    scores = einsum("bgsd,bugd->bgsu", grouped, k) * q.shape[2] ** -0.5
    high = jnp.max(scores, -1, keepdims=True)
    weights = jnp.exp(scores - high)
    seen = einsum("bgsu,bugd->bgsd", weights.astype(jnp.bfloat16), v)
    return jnp.concatenate([seen, jnp.sum(weights, -1, keepdims=True), high], -1)


def together(parts):
    seen, total, high = parts[..., :-2], parts[..., -2:-1], parts[..., -1:]
    scale = jnp.exp(high - jnp.max(high, 0))
    return (jnp.sum(seen * scale, 0) / jnp.sum(total * scale, 0)).astype(jnp.bfloat16)


def solution(mesh):
    def step(q, k, v):
        return together(lax.all_gather(part_of(q, k, v), "sp")).reshape(q.shape)

    return jax.shard_map(
        step,
        mesh=mesh,
        in_specs=(P("dp", None, None), P("dp", "sp", None, None), P("dp", "sp", None, None)),
        out_specs=P("dp", None, None),
        check_vma=False,
    )
```

profile of v0, /device:TPU:96, one launch (start us, length us, event | category | flops | bytes accessed | tf_op | source)
XLA Modules:
  0.0 267.0 jit_solution(10044619646584770485)
XLA Ops:
  6.5 0.0 all-gather.3.cloned.1.call-start
  6.6 22.7 %fusion.3 = f32[32,64,1,128]{3,2,1,0:T(1,128)S(1)} fusion(bf16[32,128,64,112]{1,3,2,0:T(8,128)(2,1)} %param.4, bf16[32,64,112,1]{2,1,0,3:T(8,128)(2,1)} %bitcast.18), kind=kOutput, calls=%fused_computation.6 | convolution fusion | flops 58720256 | bytes 60227584 | tf_op jit(solution)/shard_map/bgsd,bugd->bgsu/dot_general | solution.py:8
  29.3 0.4 multiply_reduce_fusion
  29.6 0.7 fusion.7
  30.3 35.6 %fusion.1 = f32[32,64,1,112]{3,2,1,0:T(1,128)S(1)} fusion(bf16[32,128,64,112]{1,3,2,0:T(8,128)(2,1)} %param.5, bf16[32,64,128,1]{2,1,0,3:T(8,128)(2,1)S(1)} %get-tuple-element.7), kind=kOutput, calls=%fused_computation.4 | convolution fusion | flops 58720256 | bytes 60162048 | tf_op jit(solution)/shard_map/bgsu,bugd->bgsd/dot_general | solution.py:8
  65.9 1.1 copy.10
  67.0 1.5 pad_maximum_fusion
  68.5 0.1 all-gather.3.cloned.1.call-update
  68.5 175.8 %all-gather.3.cloned.1.call-done = f32[512,64,1,114]{1,0,3,2:T(8,128)} async-done(((f32[32,64,1,114]{1,0,3,2:T(8,128)}), f32[512,64,1,114]{1,0,3,2:T(8,128)}) %all-gather.3.cloned.1.call-update) | async-done | bytes 14942224 | tf_op jit(solution)/shard_map/all_gather | solution.py:28
  244.3 1.0 slice_reduce_fusion
  245.3 1.1 fusion.8
  246.4 11.8 %fusion = f32[32,64,112]{1,0,2:T(8,128)S(1)} fusion(f32[16,32,64,1,114]{2,1,0,4,3:T(8,128)} %bitcast.15, f32[16,32,64]{2,1,0:T(8,128)S(1)} %get-tuple-element.6), kind=kLoop, calls=%fused_computation.1 | loop fusion | flops 7110656 | bytes 15728640 | tf_op jit(solution)/shard_map/reduce_sum | solution.py:23
  258.2 0.2 divide_convert_fusion
  258.4 1.7 copy.6
Async XLA Ops:
  6.5 237.8 %all-gather.3.cloned.1.call-start = ((), (), s32[]{:S(2)}) async-start(), calls=%async_computation | async-start | bytes 31752192 | tf_op jit(solution)/shard_map/all_gather | solution.py:28
Sparse Core Ops, SparseCore 0:
  68.7 175.5 all-gather.2
where the time goes:
time: 268 us; the launch traced here: 267 us
  waiting for transfers between devices  176 us (66%)
  matrix products  58.3 us (22%)
  other arithmetic  16.5 us (6%)
  between operations  13.4 us (5%)
  local copies, waits for them, and re-layouts  2.86 us (1%)
    all_gather x1, waiting for transfers between devices, step(): return together(lax.all_gather(part_of(q, k, v), 'sp')).reshape(q.shape)  176 us
    dot_general x2, matrix products, einsum(): return jnp.einsum(form, a.astype(jnp.float32), b.astype(jnp.float32))  58.3 us
    reduce_sum x1, other arithmetic, together(): jnp.sum(seen * scale, 0) / jnp.sum(total * scale, 0)  11.8 us
  transfers between devices with their start and end apart: 1, of which 1 were waited for; matrix products, arithmetic and copies ran while one was open for 0% of the time, Pallas kernels for 0%

commit v1 on v0

v1 whole, which is shorter than its diff:
```python
import functools

import jax
import jax.numpy as jnp
from jax import lax
from jax.experimental import pallas as pl
from jax.experimental.pallas import tpu as pltpu
from jax.sharding import PartitionSpec as P

ROWS = 16
LANES = 128
LAG = 2
BF16, F32 = jnp.bfloat16, jnp.float32


def iota(shape, dim):
    return lax.broadcasted_iota(jnp.int32, shape, dim)


def kernel(
    n, batch, heads, head,
    q_hbm, k_hbm, v_hbm, out_hbm,
    q_s, kbuf, vbuf, rep, rep_t, mask, qbd, probs, stats, factor, part, recv, done,
    q_sem, k_sem, v_sem, own_sem, st_send, st_recv, rs_send, rs_recv, ag_send, ag_recv,
):
    me = lax.axis_index("sp")
    seqs = n * ROWS // heads
    chunks = batch // seqs
    slots = kbuf.shape[0]
    flat = ROWS * head
    units = heads // ROWS
    scale = head**-0.5

    def fetch(src, buf, sem, b):
        slot = lax.rem(b, slots)
        return pltpu.make_async_copy(src.at[b], buf.at[slot], sem.at[slot])

    def remote(src, dst, send, rcv, peer):
        return pltpu.make_async_remote_copy(
            src_ref=src, dst_ref=dst, send_sem=send, recv_sem=rcv,
            device_id={"sp": peer}, device_id_type=pl.DeviceIdType.MESH,
        )

    get_q = pltpu.make_async_copy(q_hbm, q_s, q_sem)
    get_q.start()
    for b in range(slots):
        fetch(k_hbm, kbuf, k_sem, b).start()
    for b in range(slots):
        fetch(v_hbm, vbuf, v_sem, b).start()

    barrier = pltpu.get_barrier_semaphore()
    for hop in range(1, n):
        pl.semaphore_signal(
            barrier, inc=1, device_id={"sp": lax.rem(me + hop, n)}, device_id_type=pl.DeviceIdType.MESH
        )

    rep[...] = (lax.rem(iota(rep.shape, 1), head) == iota(rep.shape, 0)).astype(F32).astype(BF16)
    rep_t[...] = (lax.rem(iota(rep_t.shape, 0), head) == iota(rep_t.shape, 1)).astype(F32).astype(BF16)
    low = iota(mask.shape, 0) * head
    col = iota(mask.shape, 1)
    mask[...] = jnp.where((col >= low) & (col < low + head), 1.0, 0.0).astype(BF16)
    get_q.wait()
    pl.semaphore_wait(barrier, n - 1)

    def spread(c):
        rows = seqs * heads
        q = q_s[pl.ds(c * seqs, seqs)].reshape(rows, head)
        wide = jnp.dot(q, rep[...], preferred_element_type=F32).astype(BF16)
        m = mask[...]
        for r in range(rows // ROWS):
            qbd[pl.ds(r * ROWS, ROWS), :] = wide[r * ROWS : (r + 1) * ROWS] * m

    def pair_of(buf, slot, j):
        return jnp.concatenate(
            [buf[slot, pl.ds((2 * j + i) * flat, flat), :] for i in range(2)], axis=1
        )

    def scores(c, i, tile):
        b = c * seqs + i
        slot = lax.rem(b, slots)
        lane = iota((8, LANES), 1)
        for j in range(units // 2):
            lhs = qbd[pl.ds(i * heads + 2 * j * ROWS, 2 * ROWS), :]
            both = jnp.dot(lhs, pair_of(kbuf, slot, j), preferred_element_type=F32) * scale
            s = jnp.concatenate([both[:ROWS, :LANES], both[ROWS:, LANES:]], axis=0)
            high = jnp.max(s, -1, keepdims=True)
            p = jnp.exp(s - high)
            total = jnp.sum(p, -1, keepdims=True)
            probs[b, pl.ds(2 * j * ROWS, 2 * ROWS), :] = p
            for t in range(2 * ROWS // 8):
                at = i * (heads // 8) + 2 * j * ROWS // 8 + t
                tile = jnp.where(lane == at, high[8 * t : 8 * t + 8], tile)
                tile = jnp.where(lane == at + LANES // 2, total[8 * t : 8 * t + 8], tile)
        return tile

    def send_stats(c):
        for hop in range(1, n):
            here = stats.at[c, me]
            remote(here, here, st_send.at[c], st_recv.at[c], lax.rem(me + hop, n)).start()

    def join_stats(c):
        few = stats.at[c, pl.ds(0, n - 1)]
        remote(few, few, st_send.at[c], st_recv.at[c], me).wait_recv()
        high = stats[c, 0]
        for j in range(1, n):
            high = jnp.maximum(high, stats[c, j])
        total = jnp.zeros_like(high)
        for j in range(n):
            t = stats[c, j]
            total = total + pltpu.roll(t, LANES // 2, 1) * jnp.exp(t - high)
        factor[...] = jnp.exp(stats[c, me] - high) / total

    def weighted(c, i):
        b = c * seqs + i
        slot = lax.rem(b, slots)
        m = mask[...]
        f = factor[...]
        zero = jnp.zeros((ROWS, LANES), BF16)
        for j in range(units // 2):
            p = probs[b, pl.ds(2 * j * ROWS, 2 * ROWS), :]
            w = []
            for t in range(2 * ROWS // 8):
                at = i * (heads // 8) + 2 * j * ROWS // 8 + t
                w.append(p[8 * t : 8 * t + 8] * f[:, at : at + 1])
            w = jnp.concatenate(w, axis=0).astype(BF16)
            lhs = jnp.concatenate(
                [jnp.concatenate([w[:ROWS], zero], 1), jnp.concatenate([zero, w[ROWS:]], 1)], 0
            )
            seen = lax.dot_general(
                lhs, pair_of(vbuf, slot, j), (((1,), (1,)), ((), ())), preferred_element_type=F32
            ).astype(BF16)
            kept = jnp.concatenate([seen[:ROWS] * m, seen[ROWS:] * m], axis=0)
            res = jnp.dot(kept, rep_t[...], preferred_element_type=F32).astype(BF16)
            for t in range(2):
                part[c, i * units + 2 * j + t] = res[t * ROWS : (t + 1) * ROWS]

    def send_parts(c):
        for hop in range(1, n):
            peer = lax.rem(me + hop, n)
            remote(part.at[c, peer], recv.at[c, me], rs_send.at[c], rs_recv.at[c], peer).start()

    def own_out(c):
        return pltpu.make_async_copy(done.at[c], out_hbm.at[c * n + me], own_sem.at[c])

    def join_parts(c):
        few = recv.at[c, pl.ds(0, n - 1)]
        remote(few, few, rs_send.at[c], rs_recv.at[c], me).wait_recv()
        recv[c, me] = part[c, me]
        total = recv[c, 0].astype(F32)
        for j in range(1, n):
            total = total + recv[c, j].astype(F32)
        done[c] = total.astype(BF16)

    def send_result(c):
        for hop in range(1, n):
            remote(done.at[c], out_hbm.at[c * n + me], ag_send, ag_recv, lax.rem(me + hop, n)).start()
        own_out(c).start()

    def work(c, with_k, with_v):
        v = c - LAG
        if with_k:
            spread(c)
        if with_v:
            join_stats(v)
        tile = jnp.zeros((8, LANES), F32)
        for h in range(seqs // 2):
            mine = (2 * h, 2 * h + 1)
            for i in mine:
                if with_k:
                    fetch(k_hbm, kbuf, k_sem, c * seqs + i).wait()
                if with_v:
                    fetch(v_hbm, vbuf, v_sem, v * seqs + i).wait()
            for i in mine:
                if with_k:
                    tile = scores(c, i, tile)
                if with_v:
                    weighted(v, i)
            for i in mine:
                if with_k:
                    @pl.when(c * seqs + i + slots < batch)
                    def _():
                        fetch(k_hbm, kbuf, k_sem, c * seqs + i + slots).start()
                if with_v:
                    @pl.when(v * seqs + i + slots < batch)
                    def _():
                        fetch(v_hbm, vbuf, v_sem, v * seqs + i + slots).start()
        if with_k:
            stats[c, me] = tile
            send_stats(c)
        if with_v:
            send_parts(v)

            @pl.when(v >= 1)
            def _():
                join_parts(v - 1)
                send_result(v - 1)

    @pl.loop(0, LAG)
    def _(c):
        work(c, True, False)

    @pl.loop(LAG, chunks)
    def _(c):
        work(c, True, True)

    @pl.loop(chunks, chunks + LAG)
    def _(c):
        work(c, False, True)

    last = chunks - 1
    join_parts(last)
    send_result(last)
    few = out_hbm.at[pl.ds(0, chunks * (n - 1))]
    remote(few, few, ag_send, ag_recv, me).wait_recv()
    remote(few, few, ag_send, ag_recv, me).wait_send()

    @pl.loop(0, chunks)
    def _(c):
        own_out(c).wait()
        few = stats.at[c, pl.ds(0, n - 1)]
        remote(few, few, st_send.at[c], st_recv.at[c], me).wait_send()
        few = recv.at[c, pl.ds(0, n - 1)]
        remote(few, few, rs_send.at[c], rs_recv.at[c], me).wait_send()


def solution(mesh):
    n = mesh.shape["sp"]

    def step(q, k, v):
        batch, tokens, heads, head = k.shape
        flat = ROWS * head
        seqs = n * ROWS // heads
        chunks = batch // seqs
        slots = 2 * seqs
        rows_of = lambda x: x.transpose(0, 2, 3, 1).reshape(batch, heads * head, tokens)
        dma = pltpu.SemaphoreType.DMA
        out = pl.pallas_call(
            functools.partial(kernel, n, batch, heads, head),
            out_shape=jax.ShapeDtypeStruct((chunks * n, ROWS, LANES), BF16),
            in_specs=[pl.BlockSpec(memory_space=pl.ANY)] * 3,
            out_specs=pl.BlockSpec(memory_space=pl.ANY),
            scratch_shapes=[
                pltpu.VMEM((batch, heads, head), BF16),
                pltpu.VMEM((slots, heads * head, tokens), BF16),
                pltpu.VMEM((slots, heads * head, tokens), BF16),
                pltpu.VMEM((head, flat), BF16),
                pltpu.VMEM((flat, LANES), BF16),
                pltpu.VMEM((ROWS, flat), BF16),
                pltpu.VMEM((seqs * heads, flat), BF16),
                pltpu.VMEM((batch, heads, tokens), F32),
                pltpu.VMEM((chunks, n, 8, LANES), F32),
                pltpu.VMEM((8, LANES), F32),
                pltpu.VMEM((chunks, n, ROWS, LANES), BF16),
                pltpu.VMEM((chunks, n, ROWS, LANES), BF16),
                pltpu.VMEM((chunks, ROWS, LANES), BF16),
                dma, dma((slots,)), dma((slots,)), dma((chunks,)),
                dma((chunks,)), dma((chunks,)), dma((chunks,)), dma((chunks,)), dma, dma,
            ],
            compiler_params=pltpu.CompilerParams(
                collective_id=0, has_side_effects=True, vmem_limit_bytes=60 * 2**20
            ),
            cost_estimate=pl.CostEstimate(
                flops=4 * k.size, bytes_accessed=4 * k.size, transcendentals=0
            ),
        )(q, rows_of(k), rows_of(v))
        return out.reshape(batch, heads, LANES)[:, :, :head]

    return jax.shard_map(
        step,
        mesh=mesh,
        in_specs=(P("dp", None, None), P("dp", "sp", None, None), P("dp", "sp", None, None)),
        out_specs=P("dp", None, None),
        check_vma=False,
    )
```

time: 268 us -> 73.5 us (0.27)
  waiting for transfers between devices: 176 us -> 0 us
  Pallas kernels: 0 us -> 71.5 us
  matrix products: 58.3 us -> 0 us
  other arithmetic: 16.5 us -> 0 us
  between operations: 13.4 us -> 0.01 us
    all_gather x1 -> x0, waiting for transfers between devices: 176 us -> none  [step(): return together(lax.all_gather(part_of(q, k, v), 'sp')).reshape(q.shape)]
    pallas_call x0 -> x1, Pallas kernels: none -> 71.5 us  [step(): pl.pallas_call(functools.partial(kernel, n, batch, heads, head), out_shap...]
    dot_general x2 -> x0, matrix products: 58.3 us -> none  [einsum(): return jnp.einsum(form, a.astype(jnp.float32), b.astype(jnp.float32))]
    reduce_sum x2 -> x0, other arithmetic: 12.9 us -> none  [the longest x1 11.8 us: together(): jnp.sum(seen * scale, 0) / jnp.sum(total * scale, 0)]
  transfers between devices with their start and end apart: 1 -> 0, of which waited for: 1 -> 0; matrix products, arithmetic and copies ran while one was open for 0% -> 0% of each run, Pallas kernels for 0% -> 0%
where the time goes in v1:
time: 73.5 us; the launch traced here: 73.4 us
  Pallas kernels  71.5 us (97%)
  local copies, waits for them, and re-layouts  1.87 us (3%)
    pallas_call x1, Pallas kernels, step(): pl.pallas_call(functools.partial(kernel, n, batch, heads, head), out_shap...  71.5 us
    unnamed x1, local copies, waits for them, and re-layouts  1.87 us

profile of v1, /device:TPU:96, one launch (start us, length us, event | category | flops | bytes accessed | tf_op | source)
XLA Modules:
  0.0 73.4 jit_solution(5344892206802827131)
XLA Ops:
  0.0 71.5 %shard_map.37 = bf16[128,16,128]{2,1,0:T(8,128)(2,1)} custom-call(bf16[32,64,112]{2,1,0:T(8,128)(2,1)} %q_hbm.1, bf16[32,7168,128]{2,1,0:T(8,128)(2,1)} %bitcast.8, bf16[32,7168,128]{2,1,0:T(8,128)(2,1)} %bitcast.9), custom_call_target="tpu_custom_call" | custom-call | flops 117440512 | bytes 117440512 | tf_op jit(solution)/shard_map/pallas_call | solution.py:237
  71.5 1.9 %copy.5 = bf16[32,64,112]{2,1,0:T(8,128)(2,1)} copy(bf16[32,64,112]{2,1,0:T(8,128)(2,1)} %bitcast.10) | data formatting | bytes 917504

commit v2 on v1

--- a/solution.py
+++ b/solution.py
@@ -9,7 +9,8 @@
 
 ROWS = 16
 LANES = 128
-LAG = 2
+LAG = 3
+JOIN = 3
 BF16, F32 = jnp.bfloat16, jnp.float32
 
 
@@ -45,8 +46,6 @@
     get_q.start()
     for b in range(slots):
         fetch(k_hbm, kbuf, k_sem, b).start()
-    for b in range(slots):
-        fetch(v_hbm, vbuf, v_sem, b).start()
 
     barrier = pltpu.get_barrier_semaphore()
     for hop in range(1, n):
@@ -116,6 +115,7 @@
         m = mask[...]
         f = factor[...]
         zero = jnp.zeros((ROWS, LANES), BF16)
+        kept = []
         for j in range(units // 2):
             p = probs[b, pl.ds(2 * j * ROWS, 2 * ROWS), :]
             w = []
@@ -129,10 +129,13 @@
             seen = lax.dot_general(
                 lhs, pair_of(vbuf, slot, j), (((1,), (1,)), ((), ())), preferred_element_type=F32
             ).astype(BF16)
-            kept = jnp.concatenate([seen[:ROWS] * m, seen[ROWS:] * m], axis=0)
-            res = jnp.dot(kept, rep_t[...], preferred_element_type=F32).astype(BF16)
-            for t in range(2):
-                part[c, i * units + 2 * j + t] = res[t * ROWS : (t + 1) * ROWS]
+            kept += [seen[:ROWS] * m, seen[ROWS:] * m]
+        return kept
+
+    def narrow(c, i, kept):
+        res = jnp.dot(jnp.concatenate(kept, 0), rep_t[...], preferred_element_type=F32).astype(BF16)
+        for t in range(len(kept)):
+            part[c, i * units + t] = res[t * ROWS : (t + 1) * ROWS]
 
     def send_parts(c):
         for hop in range(1, n):
@@ -170,12 +173,19 @@
                     fetch(k_hbm, kbuf, k_sem, c * seqs + i).wait()
                 if with_v:
                     fetch(v_hbm, vbuf, v_sem, v * seqs + i).wait()
+            kept = []
             for i in mine:
                 if with_k:
                     tile = scores(c, i, tile)
                 if with_v:
-                    weighted(v, i)
+                    kept += weighted(v, i)
+            if with_v:
+                narrow(v, mine[0], kept)
             for i in mine:
+                if with_k and not with_v:
+                    @pl.when(c * seqs + i < slots)
+                    def _():
+                        fetch(v_hbm, vbuf, v_sem, c * seqs + i).start()
                 if with_k:
                     @pl.when(c * seqs + i + slots < batch)
                     def _():
@@ -190,10 +200,10 @@
         if with_v:
             send_parts(v)
 
-            @pl.when(v >= 1)
+            @pl.when(v >= JOIN)
             def _():
-                join_parts(v - 1)
-                send_result(v - 1)
+                join_parts(v - JOIN)
+                send_result(v - JOIN)
 
     @pl.loop(0, LAG)
     def _(c):
@@ -207,9 +217,11 @@
     def _(c):
         work(c, False, True)
 
-    last = chunks - 1
-    join_parts(last)
-    send_result(last)
+    @pl.loop(chunks - JOIN, chunks)
+    def _(c):
+        join_parts(c)
+        send_result(c)
+
     few = out_hbm.at[pl.ds(0, chunks * (n - 1))]
     remote(few, few, ag_send, ag_recv, me).wait_recv()
     remote(few, few, ag_send, ag_recv, me).wait_send()

time: 73.5 us -> 63.8 us (0.87)
  Pallas kernels: 71.5 us -> 61.8 us
    pallas_call x1, Pallas kernels: 71.5 us -> 61.8 us  [step(): pl.pallas_call(functools.partial(kernel, n, batch, heads, head), out_shap...]
where the time goes in v2:
time: 63.8 us; the launch traced here: 63.7 us
  Pallas kernels  61.8 us (97%)
  local copies, waits for them, and re-layouts  1.87 us (3%)
    pallas_call x1, Pallas kernels, step(): pl.pallas_call(functools.partial(kernel, n, batch, heads, head), out_shap...  61.8 us
    unnamed x1, local copies, waits for them, and re-layouts  1.87 us

profile of v2, /device:TPU:96, one launch (start us, length us, event | category | flops | bytes accessed | tf_op | source)
XLA Modules:
  0.0 63.7 jit_solution(403274530786641872)
XLA Ops:
  0.0 61.8 %shard_map.37 = bf16[128,16,128]{2,1,0:T(8,128)(2,1)} custom-call(bf16[32,64,112]{2,1,0:T(8,128)(2,1)} %q_hbm.1, bf16[32,7168,128]{2,1,0:T(8,128)(2,1)} %bitcast.8, bf16[32,7168,128]{2,1,0:T(8,128)(2,1)} %bitcast.9), custom_call_target="tpu_custom_call" | custom-call | flops 117440512 | bytes 117440512 | tf_op jit(solution)/shard_map/pallas_call | solution.py:249
  61.8 1.9 %copy.5 = bf16[32,64,112]{2,1,0:T(8,128)(2,1)} copy(bf16[32,64,112]{2,1,0:T(8,128)(2,1)} %bitcast.10) | data formatting | bytes 917504
